TPU v7x, 32 devices: a whole 2x2x4 slice. The times are simulated.
32 devices in a mesh: samples: 8 (over z, y), groups: 4 (over x, core).
Axes of the slice: x: 2, y: 2, z: 4, core: 2. Of those that a mesh axis runs over, the one named last changes fastest.
Arguments:
- observed: bfloat16 [128, 10240], P('samples', 'groups'), may hold values from -200 to 200
- labels: int32 [10240], P('groups'), may hold values from 0 to 31, as said below
- comp_sizes: int32 [32], P('groups'), may hold values from 128 to 512, as said below
Outputs:
- whitened: bfloat16 [128, 10240], P('samples', 'groups')
Inputs may be any that keep to these rules, and one draw needn't show every extreme that they name: Group g's columns (g * 2560 to (g + 1) * 2560 - 1) carry exactly the labels g * 8 to (g + 1) * 8 - 1, and label c stands on exactly comp_sizes[c] columns. `comp_sizes`: in every group one component has exactly 512 variables; components 2k and 2k + 1 (k = 0, 1, ...) together have exactly 640 variables.
All inputs are finite; a program needn't handle non-finite values. Where the computation divides by a largest or mean magnitude, that divisor is 1e-20 or more.
Results may differ from a plain program's by a relative error of at most 0.0038.
The roundings to bfloat16 on the way count: a program that leaves them out, or rounds other values in their place, can miss the bound.
Values may be sent and summed in bfloat16 or wider, within the bound.
A program may use at most 64 MiB of HBM per device.

v0:
```python
import jax
import jax.numpy as jnp
from jax import lax
from jax.sharding import PartitionSpec as P

CMAX = 512
ITERS = 5


shrink = 0.2
ridge = 0.5


def newton_batch(matrices):
    extent = matrices.shape[-1]
    identity = jnp.eye(extent, dtype=jnp.float32)[None]
    row_bound = jnp.max(jnp.sum(jnp.abs(matrices), axis=2), axis=1)
    current = identity / row_bound[:, None, None]
    for sweep_index in range(ITERS):
        product = jnp.einsum("kab,kbc->kac", matrices, current, precision=lax.Precision.HIGHEST)
        current = jnp.einsum(
            "kab,kbc->kac", current, 2.0 * identity - product, precision=lax.Precision.HIGHEST
        )
    return current


def shrunk_inverse(covariance, slot_sizes, average):
    extent = covariance.shape[-1]
    target = jnp.trace(covariance, axis1=1, axis2=2) / slot_sizes.astype(jnp.float32)
    diag_lift = shrink * target + ridge * average
    matrices = (1.0 - shrink) * covariance + diag_lift[:, None, None] * jnp.eye(
        extent, dtype=jnp.float32
    )[None]
    return newton_batch(matrices).astype(jnp.bfloat16)


def body(observed, labels, comp_sizes):
    row_local, width_local = observed.shape
    slot_total = comp_sizes.shape[0]
    samples_count = lax.axis_size("samples")
    groups_count = lax.axis_size("groups")
    slot_here = slot_total // samples_count
    row_count = row_local * samples_count
    local_label = labels - lax.axis_index("groups") * slot_total
    sort_order = jnp.argsort(local_label, stable=True)
    sorted_label = local_label[sort_order]
    slot_sizes = lax.dynamic_slice_in_dim(
        comp_sizes, lax.axis_index("samples") * slot_here, slot_here
    )
    starts = jnp.cumsum(comp_sizes) - comp_sizes
    offsets = jnp.arange(CMAX, dtype=jnp.int32)
    position = starts[:, None] + offsets[None, :]
    live = offsets[None, :] < comp_sizes[:, None]
    source = sort_order[jnp.minimum(position, width_local - 1)]
    source = jnp.where(live, source, width_local).reshape(slot_total * CMAX)
    padded_source = jnp.concatenate([observed, jnp.zeros((row_local, 1), jnp.bfloat16)], axis=1)
    packed = jnp.take(padded_source, source, axis=1).reshape(row_local, slot_total, CMAX)
    matches = sorted_label[:, None] == jnp.arange(slot_total, dtype=jnp.int32)[None, :]
    first_index = jnp.sum(jnp.where(matches, starts[None, :], 0), axis=1)
    placed = sorted_label * CMAX + jnp.arange(width_local, dtype=jnp.int32) - first_index
    target_column = jnp.zeros((width_local,), jnp.int32).at[sort_order].set(placed)
    column_slab = lax.all_to_all(packed, "samples", split_axis=1, concat_axis=0, tiled=True)
    slab_wide = column_slab.astype(jnp.float32)
    raw_sums = jnp.einsum("rkc,rkd->kcd", slab_wide, slab_wide, precision=lax.Precision.HIGHEST)
    energy = lax.psum(jnp.sum(jnp.trace(raw_sums, axis1=1, axis2=2)), ("samples", "groups"))
    average = energy / (row_count * width_local * groups_count)
    inverse = shrunk_inverse(raw_sums / row_count, slot_sizes, average)
    mapped = jnp.einsum(
        "rkc,kcd->rkd", slab_wide, inverse.astype(jnp.float32), precision=lax.Precision.HIGHEST
    ).astype(jnp.bfloat16)
    returned = lax.all_to_all(mapped, "samples", split_axis=0, concat_axis=1, tiled=True)
    flat_result = returned.reshape(row_local, slot_total * CMAX)
    return jnp.take(flat_result, target_column, axis=1)


def solution(mesh):
    return jax.shard_map(
        body,
        mesh=mesh,
        in_specs=(P("samples", "groups"), P("groups"), P("groups")),
        out_specs=P("samples", "groups"),
        check_vma=False,
    )
```

profile of v0, /device:TPU:0, one launch (start us, length us, event | category | flops | bytes accessed | tf_op | source)
XLA Modules:
  0.0 164.6 jit_solution(7108508053988866344)
XLA Ops:
  1.6 5.7 %sort.17 = (s32[2560]{0:T(1024)}, s32[2560]{0:T(1024)S(1)}) sort(s32[2560]{0:T(1024)S(1)} %broadcast_subtract_fusion, s32[2560]{0:T(1024)S(1)} %iota.76), dimensions={0}, to_apply=%region_0.0 | sort | flops 30720 | bytes 40960 | tf_op jit(solution)/shard_map/jit(argsort)/sort | solution.py:45
  7.4 23.0 %gather_fusion.1 = s32[4096]{0:T(1024)S(1)} fusion(s32[2560]{0:T(1024)S(1)} %get-tuple-element.6, s32[4096]{0:T(1024)S(1)} %broadcast_clamp_fusion.1), kind=kCustom, calls=%fused_computation.1 | custom fusion | bytes 49152 | tf_op jit(solution)/shard_map/gather | solution.py:54
  31.8 12.1 %gather_fusion.2 = bf16[4096,16]{1,0:T(8,128)(2,1)S(1)} fusion(bf16[16,2561]{0,1:T(8,128)(2,1)S(1)} %concatenate.3, s32[4096]{0:T(1024)S(1)} %broadcast_clamp_fusion), kind=kCustom, calls=%fused_computation.2 | custom fusion | bytes 278528 | tf_op jit(solution)/shard_map/jit(_take)/gather | solution.py:57
  44.9 7.3 %all-to-all-start = ((bf16[16,8,512]{2,0,1:T(8,128)(2,1)}), bf16[16,8,512]{2,0,1:T(8,128)(2,1)S(1)}, u32[]{:S(2)}, u32[]{:S(2)}) async-start(bf16[16,8,512]{2,0,1:T(8,128)(2,1)} %broadcast_select_fusion), calls=%async_computation | async-start | bytes 262144 | tf_op jit(solution)/shard_map/all_to_all | solution.py:62
  52.3 13.6 %gather_fusion = s32[2560]{0:T(1024)S(1)} fusion(s32[2560]{0:T(1024)S(1)} %broadcast_subtract_fusion, s32[3072]{0:T(1024)S(1)} %pad_clamp_fusion.1), kind=kCustom, calls=%fused_computation | custom fusion | bytes 30720 | tf_op jit(solution)/shard_map/gather | solution.py:46
  67.3 9.9 %scatter_custom_fusion = s32[2560]{0:T(1024)S(1)} fusion(s32[2560]{0:T(1024)S(1)} %compare_select_fusion.4, s32[2560]{0:T(1024)S(1)} %add_subtract_fusion, s32[]{:T(128)} %constant.40.clone.1), kind=kCustom, calls=%fused_computation.49 | custom fusion | bytes 10244 | tf_op jit(solution)/shard_map/scatter | solution.py:61
  77.2 1.0 select_reduce_fusion
  78.2 40.9 %psum.7 = f32[]{:T(128)} all-reduce(f32[]{:T(128)} %get-tuple-element.7), channel_id=1, replica_groups=mesh['samples'=8,'groups'=4] {'samples','groups'}, use_global_device_ids=true, to_apply=%region_6.7 | all-reduce | flops 1 | bytes 8 | tf_op jit(solution)/shard_map/psum | solution.py:65
  122.1 1.9 %select_subtract_fusion.4 = f32[512,512]{0,1:T(8,128)S(1)} fusion(f32[]{:T(128)S(6)} %divide.4, f32[512,512]{0,1:T(8,128)S(1)} %get-tuple-element.9, f32[]{:T(128)} %bitcast.11), kind=kOutput, calls=%fused_computation.9 | convolution fusion | flops 1612972032 | bytes 2097160 | tf_op jit(solution)/shard_map/kab,kbc->kac/dot_general | solution.py:20
  124.0 1.9 %fusion = f32[512,512]{1,0:T(8,128)S(1)} fusion(f32[512,512]{0,1:T(8,128)S(1)} %select_subtract_fusion.4, f32[]{:T(128)S(6)} %divide.4), kind=kOutput, calls=%fused_computation.10 | convolution fusion | flops 1611137024 | bytes 2097156 | tf_op jit(solution)/shard_map/kab,kbc->kac/dot_general | solution.py:21
  125.9 1.9 %select_subtract_fusion.3 = f32[512,512]{0,1:T(8,128)S(1)} fusion(f32[512,512]{1,0:T(8,128)S(1)} %fusion, f32[512,512]{0,1:T(8,128)S(1)} %get-tuple-element.9, f32[]{:T(128)} %bitcast.11), kind=kOutput, calls=%fused_computation.8 | convolution fusion | flops 1612447744 | bytes 3145732 | tf_op jit(solution)/shard_map/kab,kbc->kac/dot_general | solution.py:20
  127.9 1.9 %fusion.19 = f32[512,512]{1,0:T(8,128)S(1)} fusion(f32[512,512]{1,0:T(8,128)S(1)} %fusion, f32[512,512]{0,1:T(8,128)S(1)} %select_subtract_fusion.3), kind=kOutput, calls=%fused_computation.54 | convolution fusion | flops 1610612736 | bytes 3145728 | tf_op jit(solution)/shard_map/kab,kbc->kac/dot_general | solution.py:21
  129.7 1.9 %select_subtract_fusion.2 = f32[512,512]{0,1:T(8,128)S(1)} fusion(f32[512,512]{1,0:T(8,128)S(1)} %fusion.19, f32[512,512]{0,1:T(8,128)S(1)} %get-tuple-element.9, f32[]{:T(128)} %bitcast.11), kind=kOutput, calls=%fused_computation.7 | convolution fusion | flops 1612447744 | bytes 3145732 | tf_op jit(solution)/shard_map/kab,kbc->kac/dot_general | solution.py:20
  131.7 1.9 %fusion.20 = f32[512,512]{1,0:T(8,128)S(1)} fusion(f32[512,512]{1,0:T(8,128)S(1)} %fusion.19, f32[512,512]{0,1:T(8,128)S(1)} %select_subtract_fusion.2), kind=kOutput, calls=%fused_computation.55 | convolution fusion | flops 1610612736 | bytes 3145728 | tf_op jit(solution)/shard_map/kab,kbc->kac/dot_general | solution.py:21
  133.5 2.1 %select_subtract_fusion.1 = f32[512,512]{0,1:T(8,128)S(1)} fusion(f32[512,512]{1,0:T(8,128)S(1)} %fusion.20, f32[512,512]{0,1:T(8,128)S(1)} %get-tuple-element.9, f32[]{:T(128)} %bitcast.11), kind=kOutput, calls=%fused_computation.6 | convolution fusion | flops 1612447744 | bytes 3145732 | tf_op jit(solution)/shard_map/kab,kbc->kac/dot_general | solution.py:20
  135.7 1.9 %fusion.21 = f32[512,512]{1,0:T(8,128)S(1)} fusion(f32[512,512]{1,0:T(8,128)S(1)} %fusion.20, f32[512,512]{0,1:T(8,128)S(1)} %select_subtract_fusion.1), kind=kOutput, calls=%fused_computation.56 | convolution fusion | flops 1610612736 | bytes 3145728 | tf_op jit(solution)/shard_map/kab,kbc->kac/dot_general | solution.py:21
  137.6 1.9 %select_subtract_fusion = f32[512,512]{0,1:T(8,128)S(1)} fusion(f32[512,512]{1,0:T(8,128)S(1)} %fusion.21, f32[512,512]{0,1:T(8,128)S(1)} %get-tuple-element.9, f32[]{:T(128)} %bitcast.11), kind=kOutput, calls=%fused_computation.5 | convolution fusion | flops 1612447744 | bytes 3145732 | tf_op jit(solution)/shard_map/kab,kbc->kac/dot_general | solution.py:20
  139.5 1.9 %convolution_convert_fusion = bf16[512,512]{1,0:T(8,128)(2,1)S(1)} fusion(f32[512,512]{1,0:T(8,128)S(1)} %fusion.21, f32[512,512]{0,1:T(8,128)S(1)} %select_subtract_fusion), kind=kOutput, calls=%fused_computation.15 | convolution fusion | flops 1610874880 | bytes 2621440 | tf_op jit(solution)/shard_map/kab,kbc->kac/dot_general | solution.py:21
  143.0 0.7 reshape.287
  143.8 5.5 %all-to-all-start.1 = ((bf16[8,2,4096]{2,1,0:T(2,128)(2,1)}), bf16[8,2,4096]{2,1,0:T(2,128)(2,1)S(1)}, u32[]{:S(2)}, u32[]{:S(2)}) async-start(bf16[8,2,4096]{2,1,0:T(2,128)(2,1)} %reshape.287), calls=%async_computation.1 | async-start | bytes 262144 | tf_op jit(solution)/shard_map/all_to_all | solution.py:71
  149.3 7.3 %all-to-all-done.1 = bf16[8,2,4096]{2,1,0:T(2,128)(2,1)S(1)} async-done(((bf16[8,2,4096]{2,1,0:T(2,128)(2,1)}), bf16[8,2,4096]{2,1,0:T(2,128)(2,1)S(1)}, u32[]{:S(2)}, u32[]{:S(2)}) %all-to-all-start.1) | async-done | bytes 131104 | tf_op jit(solution)/shard_map/all_to_all | solution.py:71
  157.3 5.1 %gather_fusion.3 = bf16[2560,16]{1,0:T(8,128)(2,1)S(1)} fusion(bf16[16,4096]{0,1:T(8,128)(2,1)S(1)} %bitcast.58, s32[3072]{0:T(1024)S(1)} %pad_clamp_fusion), kind=kCustom, calls=%fused_computation.3 | custom fusion | bytes 174080 | tf_op jit(solution)/shard_map/jit(_take)/gather | solution.py:73
  162.4 1.3 select_bitcast_fusion
  163.7 0.9 copy.34
  (41 shorter events, 7.8 us)
Async XLA Ops:
  0.0 0.7 copy-start.2
  0.9 0.7 copy-start.1
  30.4 0.9 copy-start
  44.9 32.3 %all-to-all-start = ((bf16[16,8,512]{2,0,1:T(8,128)(2,1)}), bf16[16,8,512]{2,0,1:T(8,128)(2,1)S(1)}, u32[]{:S(2)}, u32[]{:S(2)}) async-start(bf16[16,8,512]{2,0,1:T(8,128)(2,1)} %broadcast_select_fusion), calls=%async_computation | async-start | bytes 262144 | tf_op jit(solution)/shard_map/all_to_all | solution.py:62
  143.8 12.9 %all-to-all-start.1 = ((bf16[8,2,4096]{2,1,0:T(2,128)(2,1)}), bf16[8,2,4096]{2,1,0:T(2,128)(2,1)S(1)}, u32[]{:S(2)}, u32[]{:S(2)}) async-start(bf16[8,2,4096]{2,1,0:T(2,128)(2,1)} %reshape.287), calls=%async_computation.1 | async-start | bytes 262144 | tf_op jit(solution)/shard_map/all_to_all | solution.py:71
where the time goes:
time: 165 us
  local copies, waits for them, and re-layouts  70 us (42%)
  blocking collectives  40.9 us (25%)
  matrix products  20.5 us (12%)
  starting transfers between devices  12.8 us (8%)
  other arithmetic  9.87 us (6%)
  waiting for transfers between devices  7.32 us (4%)
  between operations  3.04 us (2%)
    psum x1, blocking collectives, body(): lax.psum(jnp.sum(jnp.trace(raw_sums, axis1=1, axis2=2)), ('samples', 'gro...  40.9 us
    gather x2, local copies, waits for them, and re-layouts, body(): source = sort_order[jnp.minimum(position, width_local - 1)]  23 us
    gather x1, local copies, waits for them, and re-layouts, body(): sorted_label = local_label[sort_order]  13.6 us
    gather x2, local copies, waits for them, and re-layouts, body(): jnp.take(padded_source, source, axis=1).reshape(row_local, slot_total, CMAX)  12.5 us
    scatter x1, local copies, waits for them, and re-layouts, body(): jnp.zeros((width_local,), jnp.int32).at[sort_order].set(placed)  9.93 us
    dot_general x5, matrix products, newton_batch(): jnp.einsum('kab,kbc->kac', matrices, current, precision=lax.Precision.HIG...  9.84 us
    dot_general x5, matrix products, newton_batch(): jnp.einsum('kab,kbc->kac', current, 2.0 * identity - product, precision=l...  9.34 us
    all_to_all x1, waiting for transfers between devices, body(): lax.all_to_all(mapped, 'samples', split_axis=0, concat_axis=1, tiled=True)  7.32 us
  transfers between devices with their start and end apart: 2, of which 1 were waited for; matrix products, arithmetic and copies ran while one was open for 15% of the time, Pallas kernels for 0%

commit v1 on v0

v1 whole, which is shorter than its diff:
```python
import functools

import jax
import jax.numpy as jnp
from jax import lax
from jax.experimental import pallas as pl
from jax.experimental.pallas import tpu as pltpu
from jax.sharding import PartitionSpec as P

CMAX = 512
ITERS = 5
LANES = 128
UNROLL_LIMIT = 1024

shrink = 0.2
ridge = 0.5

BF16 = jnp.bfloat16
F32 = jnp.float32
HIGHEST = lax.Precision.HIGHEST
MESH = pl.DeviceIdType.MESH
VMEM = pl.BlockSpec(memory_space=pltpu.VMEM)


def loop(count, step, carry, unrolled):
    if unrolled:
        for i in range(count):
            carry = step(i, carry)
        return carry
    return lax.fori_loop(0, count, step, carry)


def lane_gather(values, index):
    return jnp.take_along_axis(values, index, axis=1)


def pack_kernel(
    slots, label_ref, observed_ref, packed_ref, place_ref, energy_ref, sorted_ref, low_ref, high_ref, turn_ref
):
    tiles, rows, _ = sorted_ref.shape
    first = lax.axis_index("groups") * slots
    slot = lax.broadcasted_iota(jnp.int32, (slots, LANES), 0)
    down = lax.broadcasted_iota(jnp.int32, (LANES, LANES), 0)
    across = lax.broadcasted_iota(jnp.int32, (LANES, LANES), 1)
    upto = (down <= across).astype(BF16)
    ones = jnp.ones((LANES, LANES), BF16)

    def sort_tile(t, carry):
        base, energy = carry
        label = label_ref[pl.ds(t, 1), :] - first
        equal = (label == slot).astype(F32)
        less = (label < slot).astype(F32)
        rank = jnp.dot(equal.astype(BF16), upto, preferred_element_type=F32) - 1.0
        count = jnp.dot(equal.astype(BF16), ones, preferred_element_type=F32)
        before = jnp.dot(less.astype(BF16), ones, preferred_element_type=F32)
        local = jnp.sum(equal * (before + rank), axis=0, keepdims=True).astype(jnp.int32)
        whole = slot.astype(F32) * CMAX + base + rank
        place_ref[pl.ds(t, 1), :] = jnp.sum(equal * whole, axis=0, keepdims=True).astype(jnp.int32)
        block = observed_ref[t]
        choose = (down == local).astype(BF16)
        sorted_ref[t] = lax.dot_general(
            block, choose, (((1,), (1,)), ((), ())), preferred_element_type=F32
        )
        low_ref[t] = base.astype(jnp.int32)
        high_ref[t] = (base + count).astype(jnp.int32)
        turn_ref[t] = (before - base).astype(jnp.int32)
        wide = block.astype(F32)
        square = wide * wide
        for r in range(0, rows, 8):
            energy = energy + square[r : r + 8]
        return base + count, energy

    start = (jnp.zeros((slots, LANES), F32), jnp.zeros((8, LANES), F32))
    unrolled = tiles * slots <= UNROLL_LIMIT
    _, energy = loop(tiles, sort_tile, start, unrolled)
    energy_ref[...] = energy

    lane = lax.broadcasted_iota(jnp.int32, (rows, LANES), 1)
    parts = CMAX // LANES

    def pack_slot(c, carry):
        def add_tile(t, packed):
            low = jnp.broadcast_to(low_ref[t, pl.ds(c, 1), :], (rows, LANES))
            high = jnp.broadcast_to(high_ref[t, pl.ds(c, 1), :], (rows, LANES))
            turn = jnp.broadcast_to(turn_ref[t, pl.ds(c, 1), :], (rows, LANES))
            moved = lane_gather(sorted_ref[t], (lane + turn) & (LANES - 1))
            return tuple(
                jnp.where((lane + q * LANES >= low) & (lane + q * LANES < high), moved, packed[q])
                for q in range(parts)
            )

        zero = jnp.zeros((rows, LANES), F32)
        packed = loop(tiles, add_tile, (zero,) * parts, unrolled)
        for q in range(parts):
            packed_ref[c, :, q * LANES : (q + 1) * LANES] = packed[q].astype(BF16)
        return carry

    loop(slots, pack_slot, 0, unrolled)


def unpack_kernel(place_ref, packed_ref, result_ref, wide_ref):
    tiles, rows, _ = result_ref.shape
    slots = packed_ref.shape[0]
    parts = CMAX // LANES
    unrolled = tiles * slots <= UNROLL_LIMIT

    def widen(c, carry):
        for q in range(parts):
            wide_ref[c * parts + q] = packed_ref[c, :, q * LANES : (q + 1) * LANES].astype(F32)
        return carry

    loop(slots, widen, 0, unrolled)

    def fill_tile(t, carry):
        place = jnp.broadcast_to(place_ref[pl.ds(t, 1), :], (rows, LANES))
        index = place & (LANES - 1)
        tile = place // LANES

        def take(k, value):
            return jnp.where(tile == k, lane_gather(wide_ref[k], index), value)

        value = loop(slots * parts, take, jnp.zeros((rows, LANES), F32), unrolled)
        result_ref[t] = value.astype(BF16)
        return carry

    loop(tiles, fill_tile, 0, unrolled)


def thirds(value):
    high = value.astype(BF16)
    rest = value - high.astype(F32)
    middle = rest.astype(BF16)
    low = (rest - middle.astype(F32)).astype(BF16)
    return high, middle, low


def eye(extent, value):
    down = lax.broadcasted_iota(jnp.int32, (extent, extent), 0)
    across = lax.broadcasted_iota(jnp.int32, (extent, extent), 1)
    return jnp.where(down == across, jnp.broadcast_to(value, (extent, extent)), 0.0)


def scale_and_bound(samples, gram_peak, squares, size, average):
    target = squares / samples / size
    lift = shrink * target + ridge * average
    weight = (1.0 - shrink) / samples
    return weight, lift, weight * gram_peak + lift


def whiten_rows(block, turned, inner, squares, peak, size, average, out):
    samples = block.shape[0]
    weight, lift, bound = scale_and_bound(samples, peak, squares, size, average)
    inverse_bound = 1.0 / bound
    v = inner * (weight * inverse_bound)
    e = 1.0 - lift * inverse_bound
    c = jnp.ones_like(e)
    u = d = None
    for step in range(ITERS):
        last = step == ITERS - 1
        if step == 0:
            new_d = eye(samples, -c)
            new_u = eye(samples, 2.0 * e) - v
        elif step == 1:
            new_d = v - c * u - eye(samples, 1.0 + e)
        else:
            new_d = (1.0 + e) * d - c * u - jnp.dot(d, v, precision=HIGHEST, preferred_element_type=F32)
        if not last:
            if step > 0:
                new_u = 2.0 * e * u - jnp.dot(u, v, precision=HIGHEST, preferred_element_type=F32)
            v = 2.0 * e * v - jnp.dot(v, v, precision=HIGHEST, preferred_element_type=F32)
            u = new_u
        d = new_d
        c = c * (1.0 + e)
        e = e * e
    mixed = sum(jnp.dot(piece, block, preferred_element_type=F32) for piece in reversed(thirds(d)))
    mixed = mixed * (weight * inverse_bound)
    width = block.shape[1]
    stacked = jnp.concatenate(thirds(mixed), axis=0)
    wide_turned = jnp.concatenate([turned] * 3, axis=1)
    inverse = jnp.dot(wide_turned, stacked, preferred_element_type=F32) * inverse_bound
    inverse = (inverse + eye(width, c * inverse_bound)).astype(BF16)
    out(jnp.dot(block, inverse, preferred_element_type=F32).astype(BF16))


def whiten_columns(block, gram_ref, current_ref, squares, peak, size, average, out):
    samples, width = block.shape
    weight, lift, bound = scale_and_bound(samples, peak, squares, size, average)
    gram_ref[...] = weight * gram_ref[...] + eye(width, lift)
    current_ref[...] = eye(width, 1.0 / bound)

    def sweep(i, carry):
        current = current_ref[...]
        product = jnp.dot(gram_ref[...], current, precision=HIGHEST, preferred_element_type=F32)
        current_ref[...] = jnp.dot(
            current, eye(width, jnp.full((1, 1), 2.0, F32)) - product, precision=HIGHEST, preferred_element_type=F32
        )
        return carry

    lax.fori_loop(0, ITERS, sweep, 0)
    out(jnp.dot(block, current_ref[...].astype(BF16), preferred_element_type=F32).astype(BF16))


def exchange_kernel(
    samples_count,
    groups_count,
    entries,
    size_ref,
    packed_ref,
    energy_ref,
    back_ref,
    held_ref,
    done_ref,
    group_ref,
    total_ref,
    all_ref,
    *rest,
):
    *work, group_send, group_recv, total_send, total_recv, out_send, out_recv, back_send, back_recv = rest
    me = lax.axis_index("samples")
    group = lax.axis_index("groups")
    _, slot_here, rows, width = packed_ref.shape
    samples = samples_count * rows

    def ahead(k):
        return lax.rem(me + k, samples_count)

    def behind(k):
        return lax.rem(me + samples_count - k, samples_count)

    def copy(source, target, send, recv, sample, other):
        return pltpu.make_async_remote_copy(
            src_ref=source,
            dst_ref=target,
            send_sem=send,
            recv_sem=recv,
            device_id=(sample, other),
            device_id_type=MESH,
        )

    barrier = pltpu.get_barrier_semaphore()
    for k in range(1, samples_count):
        pl.semaphore_signal(barrier, inc=1, device_id=(ahead(k), group), device_id_type=MESH)
    for k in range(1, groups_count):
        other = lax.rem(group + k, groups_count)
        pl.semaphore_signal(barrier, inc=1, device_id=(me, other), device_id_type=MESH)
    held_ref[0] = packed_ref[me]
    pl.semaphore_wait(barrier, samples_count + groups_count - 2)

    group_copies = [
        copy(
            energy_ref,
            group_ref.at[k - 1],
            group_send.at[k - 1],
            group_recv.at[k - 1],
            me,
            lax.rem(group + k, groups_count),
        )
        for k in range(1, groups_count)
    ]
    out_copies = [
        copy(packed_ref.at[ahead(k)], held_ref.at[k], out_send.at[k - 1], out_recv.at[k - 1], ahead(k), group)
        for k in range(1, samples_count)
    ]
    total_copies = [
        copy(total_ref, all_ref.at[k - 1], total_send.at[k - 1], total_recv.at[k - 1], ahead(k), group)
        for k in range(1, samples_count)
    ]
    back_copies = [
        copy(done_ref.at[k], back_ref.at[me], back_send.at[k - 1], back_recv.at[me], behind(k), group)
        for k in range(1, samples_count)
    ]
    for item in group_copies + out_copies:
        item.start()
    for item in group_copies:
        item.wait_recv()
    total = energy_ref[...]
    for k in range(groups_count - 1):
        total = total + group_ref[k]
    total_ref[...] = total
    for item in total_copies:
        item.start()
    for item in out_copies:
        item.wait_recv()

    average = None
    for h in range(slot_here):
        block = held_ref[:, h].reshape(samples, width)
        turned = block.T
        wide = block.astype(F32)
        squares = jnp.sum(jnp.sum(wide * wide, axis=0, keepdims=True), axis=1, keepdims=True)
        sums = jnp.zeros((1, width), F32)
        for r in range(0, width, LANES):
            part = jnp.dot(turned[r : r + LANES], block, preferred_element_type=F32)
            if work:
                work[0][r : r + LANES, :] = part
            sums = sums + jnp.sum(jnp.abs(part), axis=0, keepdims=True)
        peak = jnp.max(sums, axis=1, keepdims=True)
        if not work:
            inner = lax.dot_general(block, block, (((1,), (1,)), ((), ())), preferred_element_type=F32)
        if average is None:
            for item in total_copies:
                item.wait_recv()
            for k in range(samples_count - 1):
                total = total + all_ref[k]
            energy = jnp.sum(jnp.sum(total, axis=0, keepdims=True), axis=1, keepdims=True)
            average = energy / entries
        size = jnp.full((1, 1), size_ref[me * slot_here + h], jnp.int32).astype(F32)

        def out(value):
            done_ref[:, h] = value.reshape(samples_count, rows, width)

        if work:
            whiten_columns(block, work[0], work[1], squares, peak, size, average, out)
        else:
            whiten_rows(block, turned, inner, squares, peak, size, average, out)

    for item in back_copies:
        item.start()
    back_ref[me] = done_ref[0]
    for k in range(1, samples_count):
        copy(
            done_ref.at[k], back_ref.at[ahead(k)], back_send.at[k - 1], back_recv.at[ahead(k)], ahead(k), group
        ).wait_recv()
    for item in group_copies + out_copies + total_copies + back_copies:
        item.wait_send()


def body(observed, labels, comp_sizes):
    rows, width = observed.shape
    slots = comp_sizes.shape[0]
    samples_count = lax.axis_size("samples")
    groups_count = lax.axis_size("groups")
    slot_here = slots // samples_count
    tiles = width // LANES
    samples = rows * samples_count
    tiled = observed.reshape(rows, tiles, LANES).transpose(1, 0, 2)
    packed, place, energy = pl.pallas_call(
        functools.partial(pack_kernel, slots),
        out_shape=(
            jax.ShapeDtypeStruct((slots, rows, CMAX), BF16),
            jax.ShapeDtypeStruct((tiles, LANES), jnp.int32),
            jax.ShapeDtypeStruct((8, LANES), F32),
        ),
        in_specs=[VMEM] * 2,
        out_specs=(VMEM,) * 3,
        scratch_shapes=[pltpu.VMEM((tiles, rows, LANES), F32)]
        + [pltpu.VMEM((tiles, slots, LANES), jnp.int32)] * 3,
        compiler_params=pltpu.CompilerParams(vmem_limit_bytes=56 * 2**20),
        name="pack",
    )(labels.reshape(tiles, LANES), tiled)

    kind = pltpu.SemaphoreType.DMA
    work = [pltpu.VMEM((CMAX, CMAX), F32)] * 2 if samples >= CMAX else []
    back = pl.pallas_call(
        functools.partial(
            exchange_kernel, samples_count, groups_count, float(samples * width * groups_count)
        ),
        out_shape=jax.ShapeDtypeStruct((samples_count, slot_here, rows, CMAX), BF16),
        in_specs=[pl.BlockSpec(memory_space=pltpu.SMEM), VMEM, VMEM],
        out_specs=VMEM,
        scratch_shapes=[
            pltpu.VMEM((samples_count, slot_here, rows, CMAX), BF16),
            pltpu.VMEM((samples_count, slot_here, rows, CMAX), BF16),
            pltpu.VMEM((groups_count - 1, 8, LANES), F32),
            pltpu.VMEM((8, LANES), F32),
            pltpu.VMEM((samples_count - 1, 8, LANES), F32),
            *work,
            kind((groups_count - 1,)),
            kind((groups_count - 1,)),
            kind((samples_count - 1,)),
            kind((samples_count - 1,)),
            kind((samples_count - 1,)),
            kind((samples_count - 1,)),
            kind((samples_count - 1,)),
            kind((samples_count,)),
        ],
        compiler_params=pltpu.CompilerParams(
            collective_id=0, has_side_effects=True, vmem_limit_bytes=56 * 2**20
        ),
        name="exchange",
    )(comp_sizes, packed.reshape(samples_count, slot_here, rows, CMAX), energy)

    result = pl.pallas_call(
        unpack_kernel,
        out_shape=jax.ShapeDtypeStruct((tiles, rows, LANES), BF16),
        in_specs=[VMEM] * 2,
        out_specs=VMEM,
        scratch_shapes=[pltpu.VMEM((slots * CMAX // LANES, rows, LANES), F32)],
        compiler_params=pltpu.CompilerParams(vmem_limit_bytes=56 * 2**20),
        name="unpack",
    )(place, back.reshape(slots, rows, CMAX))
    return result.transpose(1, 0, 2).reshape(rows, width)


def solution(mesh):
    return jax.shard_map(
        body,
        mesh=mesh,
        in_specs=(P("samples", "groups"), P("groups"), P("groups")),
        out_specs=P("samples", "groups"),
        check_vma=False,
    )
```

time: 165 us -> 34.1 us (0.21)
  local copies, waits for them, and re-layouts: 70 us -> 3.06 us
  blocking collectives: 40.9 us -> 0 us
  Pallas kernels: 0 us -> 30.7 us
  matrix products: 20.5 us -> 0 us
  starting transfers between devices: 12.8 us -> 0 us
  other arithmetic: 9.87 us -> 0 us
  waiting for transfers between devices: 7.32 us -> 0 us
  between operations: 3.04 us -> 0.01 us
    gather x6 -> x0, local copies, waits for them, and re-layouts: 54.2 us -> none  [the longest x2 23 us: body(): source = sort_order[jnp.minimum(position, width_local - 1)]]
    psum x1 -> x0, blocking collectives: 40.9 us -> none  [body(): lax.psum(jnp.sum(jnp.trace(raw_sums, axis1=1, axis2=2)), ('samples', 'gro...]
    pallas_call x0 -> x3, Pallas kernels: none -> 30.7 us  [the longest x1 22.7 us: body(): pl.pallas_call(functools.partial(exchange_kernel, samples_count, groups_c...]
    dot_general x12 -> x0, matrix products: 20.5 us -> none  [the longest x5 9.84 us: newton_batch(): jnp.einsum('kab,kbc->kac', matrices, current, precision=lax.Precision.HIG...]
    all_to_all x2 -> x0, starting transfers between devices: 12.8 us -> none  [the longest x1 7.31 us: body(): lax.all_to_all(packed, 'samples', split_axis=1, concat_axis=0, tiled=True)]
    scatter x1 -> x0, local copies, waits for them, and re-layouts: 9.93 us -> none  [body(): jnp.zeros((width_local,), jnp.int32).at[sort_order].set(placed)]
    all_to_all x2 -> x0, waiting for transfers between devices: 7.32 us -> none  [the longest x1 7.32 us: body(): lax.all_to_all(mapped, 'samples', split_axis=0, concat_axis=1, tiled=True)]
    sort x1 -> x0, other arithmetic: 5.74 us -> none  [body(): sort_order = jnp.argsort(local_label, stable=True)]
  transfers between devices with their start and end apart: 2 -> 0, of which waited for: 1 -> 0; matrix products, arithmetic and copies ran while one was open for 15% -> 0% of each run, Pallas kernels for 0% -> 0%
where the time goes in v1:
time: 34.1 us; the launch traced here: 33.8 us
  Pallas kernels  30.7 us (90%)
  local copies, waits for them, and re-layouts  3.06 us (9%)
    pallas_call x1, Pallas kernels, body(): pl.pallas_call(functools.partial(exchange_kernel, samples_count, groups_c...  22.7 us
    pallas_call x1, Pallas kernels, body(): pl.pallas_call(functools.partial(pack_kernel, slots), out_shape=(jax.Shap...  5.69 us
    pallas_call x1, Pallas kernels, body(): pl.pallas_call(unpack_kernel, out_shape=jax.ShapeDtypeStruct((tiles, rows...  2.36 us
    reshape x1, local copies, waits for them, and re-layouts, body(): return result.transpose(1, 0, 2).reshape(rows, width)  1.53 us
    unnamed x2, local copies, waits for them, and re-layouts  0.89 us

profile of v1, /device:TPU:0, one launch (start us, length us, event | category | flops | bytes accessed | tf_op | source)
XLA Modules:
  0.0 33.8 jit_solution(7760506526766715789)
XLA Ops:
  0.0 0.0 copy-start
  0.0 0.9 %copy-done = bf16[16,2560]{1,0:T(8,128)(2,1)S(1)} copy-done((bf16[16,2560]{1,0:T(8,128)(2,1)S(1)}, bf16[16,2560]{1,0:T(8,128)(2,1)}, u32[]{:S(2)}) %copy-start) | copy-done | bytes 81944
  0.9 0.6 %bitcast_bitcast_fusion.observed_ref = bf16[20,16,128]{2,1,0:T(8,128)(2,1)} fusion(bf16[16,2560]{1,0:T(8,128)(2,1)S(1)} %copy-done), kind=kLoop, calls=%fused_computation.1 | loop fusion | bytes 163840 | tf_op jit(solution)/shard_map/transpose | solution.py:336
  1.5 5.7 %pack.1 = (bf16[8,16,512]{2,1,0:T(8,128)(2,1)}, s32[20,128]{1,0:T(8,128)}, f32[8,128]{1,0:T(8,128)}) custom-call(s32[20,128]{1,0:T(8,128)} %bitcast.18, bf16[20,16,128]{2,1,0:T(8,128)(2,1)} %bitcast_bitcast_fusion.observed_ref), custom_call_target="tpu_custom_call" | custom-call | tf_op jit(solution)/shard_map/pack/pallas_call | solution.py:337
  7.2 22.7 %exchange.1 = bf16[8,1,16,512]{3,2,1,0:T(8,128)(2,1)} custom-call(s32[8]{0:T(128)} %size_ref.1, bf16[8,1,16,512]{3,2,1,0:T(8,128)(2,1)} %bitcast.17, f32[8,128]{1,0:T(8,128)} %get-tuple-element.10.energy_ref), custom_call_target="tpu_custom_call" | custom-call | tf_op jit(solution)/shard_map/exchange/pallas_call | solution.py:354
  29.9 2.4 %unpack.1 = bf16[20,16,128]{2,1,0:T(8,128)(2,1)} custom-call(s32[20,128]{1,0:T(8,128)} %get-tuple-element.8.place_ref, bf16[8,16,512]{2,1,0:T(8,128)(2,1)} %bitcast.16), custom_call_target="tpu_custom_call" | custom-call | tf_op jit(solution)/shard_map/unpack/pallas_call | solution.py:383
  32.3 1.5 %copy_bitcast_fusion = bf16[16,2560]{1,0:T(8,128)(2,1)} fusion(bf16[20,16,128]{2,1,0:T(8,128)(2,1)} %unpack.1), kind=kLoop, calls=%fused_computation | loop fusion | bytes 163840 | tf_op jit(solution)/shard_map/reshape | solution.py:392
Async XLA Ops:
  0.0 0.9 %copy-start = (bf16[16,2560]{1,0:T(8,128)(2,1)S(1)}, bf16[16,2560]{1,0:T(8,128)(2,1)}, u32[]{:S(2)}) copy-start(bf16[16,2560]{1,0:T(8,128)(2,1)} %param.3) | copy-start | bytes 245764

commit v2 on v1

v2 whole, which is shorter than its diff:
```python
import functools

import jax
import jax.numpy as jnp
from jax import lax
from jax.experimental import pallas as pl
from jax.experimental.pallas import tpu as pltpu
from jax.sharding import PartitionSpec as P

CMAX = 512
ITERS = 5
LANES = 128
UNROLL_LIMIT = 1024

shrink = 0.2
ridge = 0.5

BF16 = jnp.bfloat16
F32 = jnp.float32
HIGHEST = lax.Precision.HIGHEST
MESH = pl.DeviceIdType.MESH
VMEM = pl.BlockSpec(memory_space=pltpu.VMEM)


def loop(count, step, carry, unrolled):
    if unrolled:
        for i in range(count):
            carry = step(i, carry)
        return carry
    return lax.fori_loop(0, count, step, carry)


def lane_gather(values, index):
    return jnp.take_along_axis(values, index, axis=1)


def thirds(value):
    high = value.astype(BF16)
    rest = value - high.astype(F32)
    middle = rest.astype(BF16)
    low = (rest - middle.astype(F32)).astype(BF16)
    return high, middle, low


def eye(extent, value):
    down = lax.broadcasted_iota(jnp.int32, (extent, extent), 0)
    across = lax.broadcasted_iota(jnp.int32, (extent, extent), 1)
    return jnp.where(down == across, jnp.broadcast_to(value, (extent, extent)), 0.0)


def scale_and_bound(samples, gram_peak, squares, size, average):
    target = squares / samples / size
    lift = shrink * target + ridge * average
    weight = (1.0 - shrink) / samples
    return weight, lift, weight * gram_peak + lift


def whiten_rows(block, turned, inner, squares, peak, size, average, out):
    samples = block.shape[0]
    weight, lift, bound = scale_and_bound(samples, peak, squares, size, average)
    inverse_bound = 1.0 / bound
    v = inner * (weight * inverse_bound)
    e = 1.0 - lift * inverse_bound
    c = jnp.ones_like(e)
    u = d = None
    for step in range(ITERS):
        last = step == ITERS - 1
        if step == 0:
            new_d = eye(samples, -c)
            new_u = eye(samples, 2.0 * e) - v
        elif step == 1:
            new_d = v - c * u - eye(samples, 1.0 + e)
        else:
            new_d = (1.0 + e) * d - c * u - jnp.dot(d, v, precision=HIGHEST, preferred_element_type=F32)
        if not last:
            if step > 0:
                new_u = 2.0 * e * u - jnp.dot(u, v, precision=HIGHEST, preferred_element_type=F32)
            v = 2.0 * e * v - jnp.dot(v, v, precision=HIGHEST, preferred_element_type=F32)
            u = new_u
        d = new_d
        c = c * (1.0 + e)
        e = e * e
    mixed = sum(jnp.dot(piece, block, preferred_element_type=F32) for piece in reversed(thirds(d)))
    mixed = mixed * (weight * inverse_bound)
    width = block.shape[1]
    stacked = jnp.concatenate(thirds(mixed), axis=0)
    wide_turned = jnp.concatenate([turned] * 3, axis=1)
    inverse = jnp.dot(wide_turned, stacked, preferred_element_type=F32) * inverse_bound
    inverse = (inverse + eye(width, c * inverse_bound)).astype(BF16)
    out(jnp.dot(block, inverse, preferred_element_type=F32).astype(BF16))


def whiten_columns(block, gram_ref, current_ref, squares, peak, size, average, out):
    samples, width = block.shape
    weight, lift, bound = scale_and_bound(samples, peak, squares, size, average)
    gram_ref[...] = weight * gram_ref[...] + eye(width, lift)
    current_ref[...] = eye(width, 1.0 / bound)

    def sweep(i, carry):
        current = current_ref[...]
        product = jnp.dot(gram_ref[...], current, precision=HIGHEST, preferred_element_type=F32)
        current_ref[...] = jnp.dot(
            current, eye(width, jnp.full((1, 1), 2.0, F32)) - product, precision=HIGHEST, preferred_element_type=F32
        )
        return carry

    lax.fori_loop(0, ITERS, sweep, 0)
    out(jnp.dot(block, current_ref[...].astype(BF16), preferred_element_type=F32).astype(BF16))


def fused_kernel(
    samples_count,
    groups_count,
    entries,
    size_ref,
    label_ref,
    observed_ref,
    result_ref,
    sorted_ref,
    low_ref,
    high_ref,
    turn_ref,
    place_ref,
    filled_ref,
    packed_ref,
    held_ref,
    done_ref,
    back_ref,
    energy_ref,
    group_ref,
    total_ref,
    all_ref,
    *rest,
):
    *work, group_send, group_recv, total_send, total_recv, out_send, out_recv, back_send, back_recv = rest
    me = lax.axis_index("samples")
    group = lax.axis_index("groups")
    _, slot_here, rows, width = packed_ref.shape
    samples = samples_count * rows
    slots = samples_count * slot_here
    tiles = sorted_ref.shape[0]
    parts = width // LANES
    unrolled = tiles * slots <= UNROLL_LIMIT
    order = sorted(range(1, samples_count), key=lambda k: abs(2 * k - samples_count))

    def ahead(k):
        return lax.rem(me + k, samples_count)

    def behind(k):
        return lax.rem(me + samples_count - k, samples_count)

    def copy(source, target, send, recv, sample, other):
        return pltpu.make_async_remote_copy(
            src_ref=source,
            dst_ref=target,
            send_sem=send,
            recv_sem=recv,
            device_id=(sample, other),
            device_id_type=MESH,
        )

    def columns(t):
        return pl.ds(t * LANES if isinstance(t, int) else pl.multiple_of(t * LANES, LANES), LANES)

    barrier = pltpu.get_barrier_semaphore()
    for k in range(1, samples_count):
        pl.semaphore_signal(barrier, inc=1, device_id=(ahead(k), group), device_id_type=MESH)
    for k in range(1, groups_count):
        other = lax.rem(group + k, groups_count)
        pl.semaphore_signal(barrier, inc=1, device_id=(me, other), device_id_type=MESH)

    first = group * slots
    slot = lax.broadcasted_iota(jnp.int32, (slots, LANES), 0)
    down = lax.broadcasted_iota(jnp.int32, (LANES, LANES), 0)
    across = lax.broadcasted_iota(jnp.int32, (LANES, LANES), 1)
    upto = (down <= across).astype(BF16)
    ones = jnp.ones((LANES, LANES), BF16)

    def sort_tile(t, carry):
        base, energy = carry
        label = label_ref[pl.ds(t, 1), :] - first
        equal = (label == slot).astype(F32)
        less = (label < slot).astype(F32)
        rank = jnp.dot(equal.astype(BF16), upto, preferred_element_type=F32) - 1.0
        count = jnp.dot(equal.astype(BF16), ones, preferred_element_type=F32)
        before = jnp.dot(less.astype(BF16), ones, preferred_element_type=F32)
        local = jnp.sum(equal * (before + rank), axis=0, keepdims=True).astype(jnp.int32)
        whole = slot.astype(F32) * CMAX + base + rank
        place_ref[pl.ds(t, 1), :] = jnp.sum(equal * whole, axis=0, keepdims=True).astype(jnp.int32)
        block = observed_ref[:, columns(t)]
        choose = (down == local).astype(BF16)
        sorted_ref[t] = lax.dot_general(
            block, choose, (((1,), (1,)), ((), ())), preferred_element_type=F32
        )
        low_ref[t] = base.astype(jnp.int32)
        high_ref[t] = (base + count).astype(jnp.int32)
        turn_ref[t] = (before - base).astype(jnp.int32)
        wide = block.astype(F32)
        square = wide * wide
        for r in range(0, rows, 8):
            energy = energy + square[r : r + 8]
        return base + count, energy

    start = (jnp.zeros((slots, LANES), F32), jnp.zeros((8, LANES), F32))
    _, total = loop(tiles, sort_tile, start, unrolled)
    energy_ref[...] = total

    lane = lax.broadcasted_iota(jnp.int32, (rows, LANES), 1)

    def pack_slot(sample, h, target):
        c = sample * slot_here + h

        def add_tile(t, packed):
            low = jnp.broadcast_to(low_ref[t, pl.ds(c, 1), :], (rows, LANES))
            high = jnp.broadcast_to(high_ref[t, pl.ds(c, 1), :], (rows, LANES))
            turn = jnp.broadcast_to(turn_ref[t, pl.ds(c, 1), :], (rows, LANES))
            moved = lane_gather(sorted_ref[t], (lane + turn) & (LANES - 1))
            return tuple(
                jnp.where((lane + q * LANES >= low) & (lane + q * LANES < high), moved, packed[q])
                for q in range(parts)
            )

        zero = jnp.zeros((rows, LANES), F32)
        packed = loop(tiles, add_tile, (zero,) * parts, unrolled)
        for q in range(parts):
            target[:, q * LANES : (q + 1) * LANES] = packed[q].astype(BF16)

    group_copies = [
        copy(
            energy_ref,
            group_ref.at[k - 1],
            group_send.at[k - 1],
            group_recv.at[k - 1],
            me,
            lax.rem(group + k, groups_count),
        )
        for k in range(1, groups_count)
    ]
    out_copies = {
        k: copy(packed_ref.at[k], held_ref.at[k], out_send.at[k - 1], out_recv.at[k - 1], ahead(k), group)
        for k in order
    }
    total_copies = [
        copy(total_ref, all_ref.at[k - 1], total_send.at[k - 1], total_recv.at[k - 1], ahead(k), group)
        for k in order
    ]
    back_copies = [
        copy(done_ref.at[k], back_ref.at[me], back_send.at[k - 1], back_recv.at[me], behind(k), group)
        for k in order
    ]

    early, late = order[:2], min(6, samples_count - 1)
    for place, k in enumerate(order):
        for h in range(slot_here):
            pack_slot(ahead(k), h, packed_ref.at[k, h])
        if k == early[-1]:
            pl.semaphore_wait(barrier, samples_count + groups_count - 2)
            for item in group_copies:
                item.start()
            for item in early:
                out_copies[item].start()
        elif place >= len(early):
            out_copies[k].start()
        if place == late - 1:
            for item in group_copies:
                item.wait_recv()
            for item in range(groups_count - 1):
                total = total + group_ref[item]
            total_ref[...] = total
            for item in total_copies:
                item.start()
    for h in range(slot_here):
        pack_slot(me, h, held_ref.at[0, h])
    for k in order:
        out_copies[k].wait_recv()

    average = None
    for h in range(slot_here):
        block = held_ref[:, h].reshape(samples, width)
        turned = block.T
        wide = block.astype(F32)
        squares = jnp.sum(jnp.sum(wide * wide, axis=0, keepdims=True), axis=1, keepdims=True)
        sums = jnp.zeros((1, width), F32)
        for r in range(0, width, LANES):
            part = jnp.dot(turned[r : r + LANES], block, preferred_element_type=F32)
            if work:
                work[0][r : r + LANES, :] = part
            sums = sums + jnp.sum(jnp.abs(part), axis=0, keepdims=True)
        peak = jnp.max(sums, axis=1, keepdims=True)
        if not work:
            inner = lax.dot_general(block, block, (((1,), (1,)), ((), ())), preferred_element_type=F32)
        if average is None:
            for item in total_copies:
                item.wait_recv()
            for k in range(samples_count - 1):
                total = total + all_ref[k]
            energy = jnp.sum(jnp.sum(total, axis=0, keepdims=True), axis=1, keepdims=True)
            average = energy / entries
        size = jnp.full((1, 1), size_ref[me * slot_here + h], jnp.int32).astype(F32)

        def out(value):
            done_ref[:, h] = value.reshape(samples_count, rows, width)

        if work:
            whiten_columns(block, work[0], work[1], squares, peak, size, average, out)
        else:
            whiten_rows(block, turned, inner, squares, peak, size, average, out)

    for item in back_copies:
        item.start()

    def fill(sample, source, opening):
        for h in range(slot_here):
            wide = [source[h, :, q * LANES : (q + 1) * LANES].astype(F32) for q in range(parts)]

            def fill_tile(t, carry):
                place = jnp.broadcast_to(place_ref[pl.ds(t, 1), :], (rows, LANES))
                place = place - (sample * slot_here + h) * CMAX
                index = place & (LANES - 1)
                if opening and h == 0:
                    value = jnp.zeros((rows, LANES), F32)
                else:
                    value = filled_ref[t]
                for q in range(parts):
                    inside = (place >= q * LANES) & (place < (q + 1) * LANES)
                    value = jnp.where(inside, lane_gather(wide[q], index), value)
                filled_ref[t] = value
                return carry

            loop(tiles, fill_tile, 0, unrolled)

    fill(me, done_ref.at[0], True)
    for k in reversed(order):
        copy(
            done_ref.at[k], back_ref.at[ahead(k)], back_send.at[k - 1], back_recv.at[ahead(k)], ahead(k), group
        ).wait_recv()
        fill(ahead(k), back_ref.at[ahead(k)], False)

    def finish(t, carry):
        result_ref[:, columns(t)] = filled_ref[t].astype(BF16)
        return carry

    loop(tiles, finish, 0, unrolled)
    for item in group_copies + list(out_copies.values()) + total_copies + back_copies:
        item.wait_send()


def body(observed, labels, comp_sizes):
    rows, width = observed.shape
    slots = comp_sizes.shape[0]
    samples_count = lax.axis_size("samples")
    groups_count = lax.axis_size("groups")
    slot_here = slots // samples_count
    tiles = width // LANES
    samples = rows * samples_count
    kind = pltpu.SemaphoreType.DMA
    table = pltpu.VMEM((tiles, slots, LANES), jnp.int32)
    wide_tiles = pltpu.VMEM((tiles, rows, LANES), F32)
    blocks = pltpu.VMEM((samples_count, slot_here, rows, CMAX), BF16)
    work = [pltpu.VMEM((CMAX, CMAX), F32)] * 2 if samples >= CMAX else []
    return pl.pallas_call(
        functools.partial(
            fused_kernel, samples_count, groups_count, float(samples * width * groups_count)
        ),
        out_shape=jax.ShapeDtypeStruct((rows, width), BF16),
        in_specs=[pl.BlockSpec(memory_space=pltpu.SMEM), VMEM, VMEM],
        out_specs=VMEM,
        scratch_shapes=[
            wide_tiles,
            table,
            table,
            table,
            pltpu.VMEM((tiles, LANES), jnp.int32),
            wide_tiles,
            blocks,
            blocks,
            blocks,
            blocks,
            pltpu.VMEM((8, LANES), F32),
            pltpu.VMEM((groups_count - 1, 8, LANES), F32),
            pltpu.VMEM((8, LANES), F32),
            pltpu.VMEM((samples_count - 1, 8, LANES), F32),
            *work,
            kind((groups_count - 1,)),
            kind((groups_count - 1,)),
            kind((samples_count - 1,)),
            kind((samples_count - 1,)),
            kind((samples_count - 1,)),
            kind((samples_count - 1,)),
            kind((samples_count - 1,)),
            kind((samples_count,)),
        ],
        compiler_params=pltpu.CompilerParams(
            collective_id=0, has_side_effects=True, vmem_limit_bytes=56 * 2**20
        ),
        name="whiten",
    )(comp_sizes, labels.reshape(tiles, LANES), observed)


def solution(mesh):
    return jax.shard_map(
        body,
        mesh=mesh,
        in_specs=(P("samples", "groups"), P("groups"), P("groups")),
        out_specs=P("samples", "groups"),
        check_vma=False,
    )
```

time: 34.1 us -> 26.5 us (0.78)
  Pallas kernels: 30.7 us -> 24.8 us
  local copies, waits for them, and re-layouts: 3.06 us -> 1.53 us
    pallas_call x3 -> x1, Pallas kernels: 30.7 us -> 24.8 us  [body(): pl.pallas_call(functools.partial(fused_kernel, samples_count, groups_coun...]
    reshape x1 -> x0, local copies, waits for them, and re-layouts: 1.53 us -> none  [body(): return result.transpose(1, 0, 2).reshape(rows, width)]
    transpose x1 -> x0, local copies, waits for them, and re-layouts: 0.65 us -> none  [body(): tiled = observed.reshape(rows, tiles, LANES).transpose(1, 0, 2)]
    unnamed x2 -> x1, local copies, waits for them, and re-layouts: 0.89 us -> 1.53 us
where the time goes in v2:
time: 26.5 us; the launch traced here: 26.3 us
  Pallas kernels  24.8 us (94%)
  local copies, waits for them, and re-layouts  1.53 us (6%)
    pallas_call x1, Pallas kernels, body(): pl.pallas_call(functools.partial(fused_kernel, samples_count, groups_coun...  24.8 us
    unnamed x1, local copies, waits for them, and re-layouts  1.53 us

profile of v2, /device:TPU:0, one launch (start us, length us, event | category | flops | bytes accessed | tf_op | source)
XLA Modules:
  0.0 26.3 jit_solution(3038003601150918292)
XLA Ops:
  0.0 24.8 %whiten.1 = bf16[16,2560]{1,0:T(8,128)(2,1)} custom-call(s32[8]{0:T(128)} %size_ref.1, s32[20,128]{1,0:T(8,128)} %bitcast.1, bf16[16,2560]{1,0:T(8,128)(2,1)} %observed_ref.1), custom_call_target="tpu_custom_call" | custom-call | tf_op jit(solution)/shard_map/whiten/pallas_call | solution.py:361
  24.8 1.5 %copy.5 = bf16[16,2560]{1,0:T(8,128)(2,1)} copy(bf16[16,2560]{1,0:T(8,128)(2,1)} %whiten.1) | data formatting | bytes 163840

commit v3 on v2

--- a/solution.py
+++ b/solution.py
@@ -40,6 +40,25 @@
     middle = rest.astype(BF16)
     low = (rest - middle.astype(F32)).astype(BF16)
     return high, middle, low
+
+
+def products(lefts, right):
+    extent = right.shape[0]
+    high, middle, low = thirds(right)
+    left_high, left_middle, left_low = thirds(jnp.concatenate(lefts, axis=0))
+    pair = jnp.concatenate([high, middle], axis=1)
+    main = jnp.dot(
+        jnp.concatenate([left_high, left_middle], axis=1),
+        jnp.concatenate([pair, pair], axis=0),
+        preferred_element_type=F32,
+    )
+    small = jnp.dot(
+        jnp.concatenate([left_high, left_low], axis=1),
+        jnp.concatenate([low, high], axis=0),
+        preferred_element_type=F32,
+    )
+    whole = (small + main[:, extent:]) + main[:, :extent]
+    return [whole[i * extent : (i + 1) * extent] for i in range(len(lefts))]
 
 
 def eye(extent, value):
@@ -64,20 +83,17 @@
     c = jnp.ones_like(e)
     u = d = None
     for step in range(ITERS):
-        last = step == ITERS - 1
+        lefts = [] if step == ITERS - 1 else [v] if step == 0 else [v, u]
+        results = products(lefts + ([d] if step > 1 else []), v)
         if step == 0:
-            new_d = eye(samples, -c)
-            new_u = eye(samples, 2.0 * e) - v
-        elif step == 1:
-            new_d = v - c * u - eye(samples, 1.0 + e)
+            d, u = eye(samples, -c), eye(samples, 2.0 * e) - v
         else:
-            new_d = (1.0 + e) * d - c * u - jnp.dot(d, v, precision=HIGHEST, preferred_element_type=F32)
-        if not last:
-            if step > 0:
-                new_u = 2.0 * e * u - jnp.dot(u, v, precision=HIGHEST, preferred_element_type=F32)
-            v = 2.0 * e * v - jnp.dot(v, v, precision=HIGHEST, preferred_element_type=F32)
-            u = new_u
-        d = new_d
+            through = results[-1] if step > 1 else -v
+            d = (1.0 + e) * d - c * u - through
+            if lefts:
+                u = 2.0 * e * u - results[1]
+        if lefts:
+            v = 2.0 * e * v - results[0]
         c = c * (1.0 + e)
         e = e * e
     mixed = sum(jnp.dot(piece, block, preferred_element_type=F32) for piece in reversed(thirds(d)))
@@ -112,12 +128,15 @@
     samples_count,
     groups_count,
     entries,
+    size_hbm,
+    label_hbm,
+    observed_hbm,
+    result_ref,
     size_ref,
     label_ref,
     observed_ref,
-    result_ref,
+    load_sem,
     sorted_ref,
-    low_ref,
     high_ref,
     turn_ref,
     place_ref,
@@ -162,6 +181,14 @@
     def columns(t):
         return pl.ds(t * LANES if isinstance(t, int) else pl.multiple_of(t * LANES, LANES), LANES)
 
+    loads = [
+        pltpu.make_async_copy(source, target, load_sem.at[i])
+        for i, (source, target) in enumerate(
+            ((label_hbm, label_ref), (observed_hbm, observed_ref), (size_hbm, size_ref))
+        )
+    ]
+    for item in loads:
+        item.start()
     barrier = pltpu.get_barrier_semaphore()
     for k in range(1, samples_count):
         pl.semaphore_signal(barrier, inc=1, device_id=(ahead(k), group), device_id_type=MESH)
@@ -169,6 +196,9 @@
         other = lax.rem(group + k, groups_count)
         pl.semaphore_signal(barrier, inc=1, device_id=(me, other), device_id_type=MESH)
 
+    for item in loads:
+        item.wait()
+
     first = group * slots
     slot = lax.broadcasted_iota(jnp.int32, (slots, LANES), 0)
     down = lax.broadcasted_iota(jnp.int32, (LANES, LANES), 0)
@@ -176,14 +206,28 @@
     upto = (down <= across).astype(BF16)
     ones = jnp.ones((LANES, LANES), BF16)
 
-    def sort_tile(t, carry):
-        base, energy = carry
+    def compare(t):
         label = label_ref[pl.ds(t, 1), :] - first
-        equal = (label == slot).astype(F32)
-        less = (label < slot).astype(F32)
+        return (label == slot).astype(F32), (label < slot).astype(F32)
+
+    def counts(equal, less):
         rank = jnp.dot(equal.astype(BF16), upto, preferred_element_type=F32) - 1.0
         count = jnp.dot(equal.astype(BF16), ones, preferred_element_type=F32)
         before = jnp.dot(less.astype(BF16), ones, preferred_element_type=F32)
+        return rank, count, before
+
+    if unrolled:
+        pairs = [compare(t) for t in range(tiles)]
+        stacked = counts(*(jnp.concatenate(items, axis=0) for items in zip(*pairs)))
+
+    def sort_tile(t, carry):
+        base, energy = carry
+        if unrolled:
+            equal = pairs[t][0]
+            rank, count, before = (item[t * slots : (t + 1) * slots] for item in stacked)
+        else:
+            equal, less = compare(t)
+            rank, count, before = counts(equal, less)
         local = jnp.sum(equal * (before + rank), axis=0, keepdims=True).astype(jnp.int32)
         whole = slot.astype(F32) * CMAX + base + rank
         place_ref[pl.ds(t, 1), :] = jnp.sum(equal * whole, axis=0, keepdims=True).astype(jnp.int32)
@@ -192,7 +236,6 @@
         sorted_ref[t] = lax.dot_general(
             block, choose, (((1,), (1,)), ((), ())), preferred_element_type=F32
         )
-        low_ref[t] = base.astype(jnp.int32)
         high_ref[t] = (base + count).astype(jnp.int32)
         turn_ref[t] = (before - base).astype(jnp.int32)
         wide = block.astype(F32)
@@ -210,13 +253,13 @@
     def pack_slot(sample, h, target):
         c = sample * slot_here + h
 
-        def add_tile(t, packed):
-            low = jnp.broadcast_to(low_ref[t, pl.ds(c, 1), :], (rows, LANES))
+        def add_tile(i, packed):
+            t = tiles - 1 - i
             high = jnp.broadcast_to(high_ref[t, pl.ds(c, 1), :], (rows, LANES))
             turn = jnp.broadcast_to(turn_ref[t, pl.ds(c, 1), :], (rows, LANES))
             moved = lane_gather(sorted_ref[t], (lane + turn) & (LANES - 1))
             return tuple(
-                jnp.where((lane + q * LANES >= low) & (lane + q * LANES < high), moved, packed[q])
+                jnp.where(lane + q * LANES < high, moved, packed[q])
                 for q in range(parts)
             )
 
@@ -249,28 +292,23 @@
         for k in order
     ]
 
-    early, late = order[:2], min(6, samples_count - 1)
-    for place, k in enumerate(order):
+    for k in order:
         for h in range(slot_here):
             pack_slot(ahead(k), h, packed_ref.at[k, h])
-        if k == early[-1]:
-            pl.semaphore_wait(barrier, samples_count + groups_count - 2)
-            for item in group_copies:
-                item.start()
-            for item in early:
-                out_copies[item].start()
-        elif place >= len(early):
-            out_copies[k].start()
-        if place == late - 1:
-            for item in group_copies:
-                item.wait_recv()
-            for item in range(groups_count - 1):
-                total = total + group_ref[item]
-            total_ref[...] = total
-            for item in total_copies:
-                item.start()
+    pl.semaphore_wait(barrier, samples_count + groups_count - 2)
+    for item in group_copies:
+        item.start()
+    for k in order:
+        out_copies[k].start()
     for h in range(slot_here):
         pack_slot(me, h, held_ref.at[0, h])
+    for item in group_copies:
+        item.wait_recv()
+    for k in range(groups_count - 1):
+        total = total + group_ref[k]
+    total_ref[...] = total
+    for item in total_copies:
+        item.start()
     for k in order:
         out_copies[k].wait_recv()
 
@@ -315,15 +353,14 @@
 
             def fill_tile(t, carry):
                 place = jnp.broadcast_to(place_ref[pl.ds(t, 1), :], (rows, LANES))
-                place = place - (sample * slot_here + h) * CMAX
                 index = place & (LANES - 1)
+                tile = (place >> (LANES.bit_length() - 1)) - (sample * slot_here + h) * parts
                 if opening and h == 0:
                     value = jnp.zeros((rows, LANES), F32)
                 else:
                     value = filled_ref[t]
                 for q in range(parts):
-                    inside = (place >= q * LANES) & (place < (q + 1) * LANES)
-                    value = jnp.where(inside, lane_gather(wide[q], index), value)
+                    value = jnp.where(tile == q, lane_gather(wide[q], index), value)
                 filled_ref[t] = value
                 return carry
 
@@ -363,11 +400,14 @@
             fused_kernel, samples_count, groups_count, float(samples * width * groups_count)
         ),
         out_shape=jax.ShapeDtypeStruct((rows, width), BF16),
-        in_specs=[pl.BlockSpec(memory_space=pltpu.SMEM), VMEM, VMEM],
+        in_specs=[pl.BlockSpec(memory_space=pltpu.HBM)] * 3,
         out_specs=VMEM,
         scratch_shapes=[
+            pltpu.SMEM(comp_sizes.shape, jnp.int32),
+            pltpu.VMEM((tiles, LANES), jnp.int32),
+            pltpu.VMEM((rows, width), BF16),
+            kind((3,)),
             wide_tiles,
-            table,
             table,
             table,
             pltpu.VMEM((tiles, LANES), jnp.int32),

time: 26.5 us -> 24.6 us (0.928)
  Pallas kernels: 24.8 us -> 22.8 us
    pallas_call x1, Pallas kernels: 24.8 us -> 22.8 us  [body(): pl.pallas_call(functools.partial(fused_kernel, samples_count, groups_coun...]
where the time goes in v3:
time: 24.6 us; the launch traced here: 24.4 us
  Pallas kernels  22.8 us (93%)
  local copies, waits for them, and re-layouts  1.53 us (6%)
    pallas_call x1, Pallas kernels, body(): pl.pallas_call(functools.partial(fused_kernel, samples_count, groups_coun...  22.8 us
    unnamed x1, local copies, waits for them, and re-layouts  1.53 us

profile of v3, /device:TPU:0, one launch (start us, length us, event | category | flops | bytes accessed | tf_op | source)
XLA Modules:
  0.0 24.4 jit_solution(1486396146723544160)
XLA Ops:
  0.0 22.8 %whiten.1 = bf16[16,2560]{1,0:T(8,128)(2,1)} custom-call(s32[8]{0:T(128)} %size_hbm.1, s32[20,128]{1,0:T(8,128)} %bitcast.1, bf16[16,2560]{1,0:T(8,128)(2,1)} %observed_hbm.1), custom_call_target="tpu_custom_call" | custom-call | tf_op jit(solution)/shard_map/whiten/pallas_call | solution.py:398
  22.8 1.5 %copy.5 = bf16[16,2560]{1,0:T(8,128)(2,1)} copy(bf16[16,2560]{1,0:T(8,128)(2,1)} %whiten.1) | data formatting | bytes 163840
